TPU v7x, 256 devices: a whole 4x4x8 slice. The times are simulated.
256 devices in a mesh: lat: 8 (over x_lo, y), lon: 32 (over z, x_hi, core).
Axes of the slice: x: 4 (x_hi: 2, x_lo: 2; x = x_hi * 2 + x_lo), y: 4, z: 8, core: 2. Of those that a mesh axis runs over, the one named last changes fastest.
Arguments:
- activations: bfloat16 [4, 32, 2880, 512], P(None, 'lat', 'lon'), may hold values from -48 to 48
- upstream: bfloat16 [4, 32, 2880, 512], P(None, 'lat', 'lon'), may hold values from -6 to 6
- master: float32 [512, 9, 512], P(('lat', 'lon')), may hold values from -0.09375 to 0.09375
- moment_one: float32 [512, 9, 512], P(('lat', 'lon')), may hold values from -2.5 to 2.5
- moment_two: float32 [512, 9, 512], P(('lat', 'lon')), may hold values from 0.01 to 1
Outputs:
- input_grad: bfloat16 [4, 32, 2880, 512], P(None, 'lat', 'lon')
- new_weights: bfloat16 [512, 9, 512], replicated
- new_master: float32 [512, 9, 512], P(('lat', 'lon'))
- new_moment_one: float32 [512, 9, 512], P(('lat', 'lon'))
- new_moment_two: float32 [512, 9, 512], P(('lat', 'lon'))
- clipped_grad: float32 [512, 9, 512], P(('lat', 'lon'))
All inputs are finite; a program needn't handle non-finite values.
Results may differ from a plain program's by a relative error of at most 0.0049.
Values may be sent and summed in bfloat16 or wider, within the bound.
No kernel may reach another device: no remote copies, remote signals or barrier semaphores. Data moves between devices by JAX's collectives and lax.ppermute only.
A program may use at most 128 MiB of HBM per device.

v0:
```python
import functools
import math
import jax
import jax.numpy as jnp
from jax import lax
from jax.sharding import Mesh
from jax.sharding import PartitionSpec as P

CIN = 512
COUT = 512
TAPS = 9
LAT = ("lat_0", "lat_1")
LAT_LON = ("lat_0", "lat_1", "lon_0", "lon_1", "lon_2")
LON = ("lon_0", "lon_1", "lon_2")
learn_rate = 0.01
beta_one = 0.9
beta_two = 0.999
adam_eps = 1e-08
decay_rate = 0.1
step_count = 10.0
norm_eps = 1e-06


def padded(block, sides, width):
    for axis, dim in sides:
        count = lax.axis_size(axis)
        forward = [(i, i + 1) for i in range(count - 1)]
        forward.append((count - 1, 0))
        backward = [(target, source) for source, target in forward]
        low = lax.ppermute(
            lax.slice_in_dim(block, block.shape[dim] - width, None, axis=dim), axis, forward
        )
        high = lax.ppermute(lax.slice_in_dim(block, 0, width, axis=dim), axis, backward)
        block = jnp.concatenate([low, block, high], axis=dim)
    return block


def sent_to_all(shard, axis):
    copies = jnp.broadcast_to(shard, (lax.axis_size(axis), *shard.shape))
    return lax.all_to_all(copies, axis, split_axis=0, concat_axis=0, tiled=True)


def joined_along(parts, dim):
    shape = list(parts.shape[1:])
    shape[dim] *= parts.shape[0]
    return jnp.moveaxis(parts, 0, dim).reshape(shape)


def gathered_copies(shard, axis, dim):
    parts = sent_to_all(shard, axis)
    return joined_along(parts, dim)


def split_up(shard, dim, count):
    before, after = (shard.shape[:dim], shard.shape[dim + 1 :])
    return jnp.moveaxis(shard.reshape(*before, count, -1, *after), dim, 0)


def sent_and_summed(shard, axis, dim):
    count = lax.axis_size(axis)
    parts = lax.all_to_all(split_up(shard, dim, count), axis, 0, 0, tiled=True)
    return jnp.sum(parts, axis=0)


def by_axis(shard, axes):
    return functools.reduce(lax.psum, axes, shard)


def mask_poles(wide_field):
    lat_index = lax.axis_index(LAT)
    lat_count = lax.axis_size(LAT)
    total_rows = wide_field.shape[1]
    row_ids = lax.broadcasted_iota(jnp.int32, (1, total_rows, 1, 1), 1)
    upper = jnp.logical_and(row_ids == 0, lat_index == 0)
    lower = jnp.logical_and(row_ids == total_rows - 1, lat_index == lat_count - 1)
    return jnp.where(jnp.logical_or(upper, lower), jnp.zeros((), wide_field.dtype), wide_field)


def pull_product(grad_wide, lat_rows, lon_cols):
    batch_rows = grad_wide.shape[0]
    out_width = grad_wide.shape[3]
    windows = []
    for tap_index in range(9):
        row_off, col_off = divmod(tap_index, 3)
        windows.append(
            grad_wide[
                :, 2 - row_off : 2 - row_off + lat_rows, 2 - col_off : 2 - col_off + lon_cols, :
            ].reshape(-1, out_width)
        )

    def pull_compute(shard_piece, first_row):
        piece_width = shard_piece.shape[0]
        summed = jnp.zeros((batch_rows * lat_rows * lon_cols, piece_width), jnp.float32)
        for tap_index in range(9):
            summed = summed + lax.dot_general(
                windows[tap_index],
                shard_piece[:, tap_index, :],
                (((1,), (1,)), ((), ())),
                preferred_element_type=jnp.float32,
            )
        return summed.reshape(batch_rows, lat_rows, lon_cols, piece_width)

    return pull_compute


def input_taps(act_wide, grad_flat, lat_rows, lon_cols):

    def input_compute(first_row, row_count):
        tap_parts = []
        for tap_index in range(9):
            row_off, col_off = divmod(tap_index, 3)
            tap_slab = act_wide[
                :, row_off : row_off + lat_rows, col_off : col_off + lon_cols, :
            ].reshape(-1, row_count)
            tap_parts.append(
                lax.dot_general(
                    tap_slab,
                    grad_flat,
                    (((0,), (0,)), ((), ())),
                    preferred_element_type=jnp.float32,
                )
            )
        return jnp.stack(tap_parts, axis=1)

    return input_compute


def per_device(activations, upstream, master, moment_one, moment_two):
    lat_rows = activations.shape[1]
    lon_cols = activations.shape[2]
    grad_flat = upstream.reshape(-1, upstream.shape[3])
    act_wide = mask_poles(padded(activations, ((LAT, 1), (LON, 2)), 1))
    grad_wide = mask_poles(padded(upstream, ((LAT, 1), (LON, 2)), 1))
    producer = pull_product(grad_wide, lat_rows, lon_cols)
    term_maker = input_taps(act_wide, grad_flat, lat_rows, lon_cols)
    old_weights = master.astype(jnp.bfloat16)
    old_block = gathered_copies(old_weights, LON, 0)
    data_sum = producer(lax.all_gather(old_block, LAT, axis=0, tiled=True), jnp.int32(0))
    input_grad = data_sum.astype(jnp.bfloat16)
    shard_rows = master.shape[0]
    lat_block = lax.psum_scatter(
        term_maker(jnp.int32(0), lax.axis_size(LAT) * (shard_rows * lax.axis_size(LON))),
        LAT,
        scatter_dimension=0,
        tiled=True,
    )
    grad_shard = sent_and_summed(lat_block, LON, 0)
    max_norm = math.sqrt(float(CIN * TAPS * COUT))
    square_sum = by_axis(jnp.sum(grad_shard * grad_shard), LAT_LON)
    clip_factor = jnp.minimum(1.0, max_norm / (jnp.sqrt(square_sum) + norm_eps))
    grad_scaled = clip_factor * grad_shard
    new_one = beta_one * moment_one + (1.0 - beta_one) * grad_scaled
    new_two = beta_two * moment_two + (1.0 - beta_two) * grad_scaled * grad_scaled
    first_hat = new_one / (1.0 - beta_one**step_count)
    second_hat = new_two / (1.0 - beta_two**step_count)
    new_master = master - learn_rate * (
        first_hat / (jnp.sqrt(second_hat) + adam_eps) + decay_rate * master
    )
    new_half = new_master.astype(jnp.bfloat16)
    lon_block = gathered_copies(new_half, LON, 0)
    new_weights = lax.all_gather(lon_block, LAT, axis=0, tiled=True)
    return (input_grad, new_weights, new_master, new_one, new_two, grad_scaled)


def solution(mesh):
    split = Mesh(mesh.devices.reshape(2, 4, 8, 2, 2), ("lat_0", "lat_1", "lon_0", "lon_1", "lon_2"))
    in_specs = (
        P(None, LAT, LON, None),
        P(None, LAT, LON, None),
        P(LAT_LON, None, None),
        P(LAT_LON, None, None),
        P(LAT_LON, None, None),
    )
    out_specs = (
        P(None, LAT, LON, None),
        P(),
        P(LAT_LON, None, None),
        P(LAT_LON, None, None),
        P(LAT_LON, None, None),
        P(LAT_LON, None, None),
    )
    return jax.shard_map(
        per_device, mesh=split, in_specs=in_specs, out_specs=out_specs, check_vma=False
    )
```

profile of v0, /device:TPU:1, one launch (start us, length us, event | category | flops | bytes accessed | tf_op | source)
XLA Modules:
  0.0 432.9 jit_solution(12576936133788156169)
XLA Ops:
  7.2 3.2 fusion.90
  18.4 3.6 collective-permute-start.5
  25.4 6.9 %collective-permute-start.2 = (bf16[4,6,1,512]{3,2,1,0:T(2,128)(2,1)S(1)}, bf16[4,6,1,512]{3,2,1,0:T(2,128)(2,1)S(1)}, u32[]{:S(2)}, u32[]{:S(2)}) collective-permute-start(bf16[4,6,1,512]{3,2,1,0:T(2,128)(2,1)S(1)} %get-tuple-element.46), channel_id=1, source_target_pairs={{0,1},{1,2},{2,3},{3,4},{4,5},{5,6},{6,7},{7,8},{8,9},{9,10},{10,1... | collective-permute-start | bytes 73736 | tf_op jit(solution)/shard_map/ppermute | solution.py:30
  34.8 4.8 %collective-permute-start.6 = (bf16[4,6,1,512]{3,2,1,0:T(2,128)(2,1)S(1)}, bf16[4,6,1,512]{3,2,1,0:T(2,128)(2,1)S(1)}, u32[]{:S(2)}, u32[]{:S(2)}) collective-permute-start(bf16[4,6,1,512]{3,2,1,0:T(2,128)(2,1)S(1)} %get-tuple-element.35), channel_id=1, source_target_pairs={{0,1},{1,2},{2,3},{3,4},{4,5},{5,6},{6,7},{7,8},{8,9},{9,10},{10,1... | collective-permute-start | bytes 73736 | tf_op jit(solution)/shard_map/ppermute | solution.py:30
  39.6 10.4 %collective-permute-start.7 = (bf16[4,6,1,512]{3,2,1,0:T(2,128)(2,1)S(1)}, bf16[4,6,1,512]{3,2,1,0:T(2,128)(2,1)S(1)}, u32[]{:S(2)}, u32[]{:S(2)}) collective-permute-start(bf16[4,6,1,512]{3,2,1,0:T(2,128)(2,1)S(1)} %get-tuple-element.36), channel_id=1, source_target_pairs={{1,0},{2,1},{3,2},{4,3},{5,4},{6,5},{7,6},{8,7},{9,8},{10,9},{11,1... | collective-permute-start | bytes 73736 | tf_op jit(solution)/shard_map/ppermute | solution.py:33
  50.1 4.9 %collective-permute-done.7 = bf16[4,6,1,512]{3,2,1,0:T(2,128)(2,1)S(1)} collective-permute-done((bf16[4,6,1,512]{3,2,1,0:T(2,128)(2,1)S(1)}, bf16[4,6,1,512]{3,2,1,0:T(2,128)(2,1)S(1)}, u32[]{:S(2)}, u32[]{:S(2)}) %collective-permute-start.7) | collective-permute-done | bytes 24608 | tf_op jit(solution)/shard_map/ppermute | solution.py:33
  55.0 2.7 maximum_select_fusion.1
  76.0 108.3 %reduce-scatter.2.cloned.1.call-done = f32[64,9,512]{2,0,1:T(8,128)} async-done(((f32[512,9,512]{2,0,1:T(8,128)}), f32[64,9,512]{2,0,1:T(8,128)}) %reduce-scatter.2.cloned.1.call-update) | async-done | bytes 1179664 | tf_op jit(solution)/shard_map/reduce_scatter | solution.py:141
  186.8 42.6 %all_to_all.15 = f32[32,2,9,512]{3,1,2,0:T(2,128)S(1)} all-to-all(f32[32,2,9,512]{3,1,2,0:T(2,128)S(1)} %copy.78), channel_id=1, replica_groups=mesh['lat_0'=2,'lat_1'=4,'lon_0'=8,'lon_1'=2,'lon_2'=2] {'lon_0','lon_1'..., dimensions={0} | all-to-all | bytes 2359296 | tf_op jit(solution)/shard_map/all_to_all | solution.py:61
  231.7 4.4 %psum.35 = f32[]{:T(128)} all-reduce(f32[]{:T(128)} %multiply_reduce_fusion), channel_id=1, replica_groups=mesh['lat_0'=2,'lat_1'=4,'lon_0'=8,'lon_1'=2,'lon_2'=2] {'lat_0'}, use_global_device_ids=true, to_apply=%region_3.4 | all-reduce | flops 1 | bytes 8 | tf_op jit(solution)/shard_map/psum | solution.py:66
  236.1 6.8 %psum.36 = f32[]{:T(128)} all-reduce(f32[]{:T(128)} %psum.35), channel_id=1, replica_groups=mesh['lat_0'=2,'lat_1'=4,'lon_0'=8,'lon_1'=2,'lon_2'=2] {'lat_1'}, use_global_device_ids=true, to_apply=%region_4.5 | all-reduce | flops 1 | bytes 8 | tf_op jit(solution)/shard_map/psum | solution.py:66
  242.9 12.3 %psum.37 = f32[]{:T(128)} all-reduce(f32[]{:T(128)} %psum.36), channel_id=1, replica_groups=mesh['lat_0'=2,'lat_1'=4,'lon_0'=8,'lon_1'=2,'lon_2'=2] {'lon_0'}, use_global_device_ids=true, to_apply=%region_5.6 | all-reduce | flops 1 | bytes 8 | tf_op jit(solution)/shard_map/psum | solution.py:66
  255.3 5.9 %psum.38 = f32[]{:T(128)} all-reduce(f32[]{:T(128)} %psum.37), channel_id=1, replica_groups=mesh['lat_0'=2,'lat_1'=4,'lon_0'=8,'lon_1'=2,'lon_2'=2] {'lon_1'}, use_global_device_ids=true, to_apply=%region_6.7 | all-reduce | flops 1 | bytes 8 | tf_op jit(solution)/shard_map/psum | solution.py:66
  261.2 11.5 %psum.39 = f32[]{:T(128)} all-reduce(f32[]{:T(128)} %psum.38), channel_id=1, replica_groups=mesh['lat_0'=2,'lat_1'=4,'lon_0'=8,'lon_1'=2,'lon_2'=2] {'lon_2'}, use_global_device_ids=true, to_apply=%region_7.8 | all-reduce | flops 1 | bytes 8 | tf_op jit(solution)/shard_map/psum | solution.py:66
  275.4 23.0 %all_to_all.16 = bf16[32,2,9,512]{3,1,2,0:T(2,128)(2,1)S(1)} all-to-all(bf16[32,2,9,512]{3,1,2,0:T(2,128)(2,1)S(1)} %broadcast_in_dim.24), channel_id=1, replica_groups=mesh['lat_0'=2,'lat_1'=4,'lon_0'=8,'lon_1'=2,'lon_2'=2] {'lon_0','lon_1'..., dimensions={0} | all-to-all | bytes 1179648 | tf_op jit(solution)/shard_map/all_to_all | solution.py:40
  300.4 23.7 %all_to_all.17 = bf16[32,2,9,512]{3,1,2,0:T(2,128)(2,1)S(1)} all-to-all(bf16[32,2,9,512]{3,1,2,0:T(2,128)(2,1)S(1)} %broadcast_in_dim.25), channel_id=1, replica_groups=mesh['lat_0'=2,'lat_1'=4,'lon_0'=8,'lon_1'=2,'lon_2'=2] {'lon_0','lon_1'..., dimensions={0} | all-to-all | bytes 1179648 | tf_op jit(solution)/shard_map/all_to_all | solution.py:40
  325.7 6.2 %fusion.87 = (bf16[4,4,90,512]{3,2,1,0:T(8,128)(2,1)}, bf16[4,4,90,512]{3,2,1,0:T(8,128)(2,1)}, bf16[4,4,90,512]{3,2,1,0:T(8,128)(2,1)}, bf16[4,4,90,512]{3,2,1,...) fusion(bf16[4,6,92,512]{3,2,1,0:T(8,128)(2,1)S(1)} %get-tuple-e, ...), kind=kLoop, calls=%fused_computation.81 | loop fusion | bytes 26542080 | tf_op jit(solution)/shard_map/slice | solution.py:86
  337.4 2.6 reshape.79
  340.0 2.5 reshape.80
  343.8 2.6 reshape.82
  346.4 2.5 reshape.83
  350.2 10.2 %all-gather.3.cloned.1.call-done = bf16[512,9,512]{2,0,1:T(8,128)(2,1)} async-done(((bf16[64,9,512]{2,0,1:T(8,128)(2,1)}), bf16[512,9,512]{2,0,1:T(8,128)(2,1)}) %all-gather.3.cloned.1.call-update) | async-done | bytes 4718608 | tf_op jit(solution)/shard_map/all_gather | solution.py:138
  376.2 45.0 %all-gather.5.cloned.1.call-done = bf16[512,9,512]{2,0,1:T(8,128)(2,1)} async-done(((bf16[64,9,512]{2,0,1:T(8,128)(2,1)}), bf16[512,9,512]{2,0,1:T(8,128)(2,1)}) %all-gather.5.cloned.1.call-update) | async-done | bytes 4718608 | tf_op jit(solution)/shard_map/all_gather | solution.py:161
  421.2 4.8 %copy.127 = bf16[512,9,512]{2,0,1:T(8,128)(2,1)} copy(bf16[512,9,512]{2,0,1:T(8,128)(2,1)} %all-gather.5.cloned.1.call-done) | data formatting | bytes 9437184
  (97 shorter events, 66.2 us)
Async XLA Ops:
  7.2 9.4 %copy-start.3 = (bf16[4,4,90,512]{3,1,2,0:T(4,128)(2,1)S(1)}, bf16[4,4,90,512]{3,1,2,0:T(4,128)(2,1)}, u32[]{:S(2)}) copy-start(bf16[4,4,90,512]{3,1,2,0:T(4,128)(2,1)} %param.5) | copy-start | bytes 4423684
  7.2 177.2 %reduce-scatter.2.cloned.1.call-start = ((), (), s32[]{:S(2)}) async-start(), calls=%async_computation.5 | async-start | bytes 10616832 | tf_op jit(solution)/shard_map/reduce_scatter | solution.py:141
  11.2 11.7 %collective-permute-start = (bf16[4,1,90,512]{3,2,1,0:T(8,128)(2,1)}, bf16[4,1,90,512]{3,2,1,0:T(8,128)(2,1)}, u32[]{:S(2)}, u32[]{:S(2)}) collective-permute-start(bf16[4,1,90,512]{3,2,1,0:T(8,128)(2,1)} %copy.110), channel_id=1, source_target_pairs={{0,32},{32,64},{64,96},{96,128},{128,160},{160,192},{192,224},{224... | collective-permute-start | bytes 1105928 | tf_op jit(solution)/shard_map/ppermute | solution.py:30
  14.2 9.8 %copy-start.4 = (bf16[4,4,90,512]{3,1,2,0:T(4,128)(2,1)S(1)}, bf16[4,4,90,512]{3,1,2,0:T(4,128)(2,1)}, u32[]{:S(2)}) copy-start(bf16[4,4,90,512]{3,1,2,0:T(4,128)(2,1)} %param.6) | copy-start | bytes 4423684
  14.2 10.1 %collective-permute-start.1 = (bf16[4,1,90,512]{3,2,1,0:T(8,128)(2,1)}, bf16[4,1,90,512]{3,2,1,0:T(8,128)(2,1)}, u32[]{:S(2)}, u32[]{:S(2)}) collective-permute-start(bf16[4,1,90,512]{3,2,1,0:T(8,128)(2,1)} %copy.111), channel_id=1, source_target_pairs={{32,0},{64,32},{96,64},{128,96},{160,128},{192,160},{224,192},{0,2... | collective-permute-start | bytes 1105928 | tf_op jit(solution)/shard_map/ppermute | solution.py:33
  18.4 14.0 %collective-permute-start.4 = (bf16[4,1,90,512]{3,2,1,0:T(8,128)(2,1)}, bf16[4,1,90,512]{3,2,1,0:T(8,128)(2,1)}, u32[]{:S(2)}, u32[]{:S(2)}) collective-permute-start(bf16[4,1,90,512]{3,2,1,0:T(8,128)(2,1)} %copy.112), channel_id=1, source_target_pairs={{0,32},{32,64},{64,96},{96,128},{128,160},{160,192},{192,224},{224... | collective-permute-start | bytes 1105928 | tf_op jit(solution)/shard_map/ppermute | solution.py:30
  18.4 15.3 %collective-permute-start.5 = (bf16[4,1,90,512]{3,2,1,0:T(8,128)(2,1)S(1)}, bf16[4,1,90,512]{3,2,1,0:T(8,128)(2,1)}, u32[]{:S(2)}, u32[]{:S(2)}) collective-permute-start(bf16[4,1,90,512]{3,2,1,0:T(8,128)(2,1)S(1)} %copy.113), channel_id=1, source_target_pairs={{32,0},{64,32},{96,64},{128,96},{160,128},{192,160},{224,192},{0,2... | collective-permute-start | bytes 1105928 | tf_op jit(solution)/shard_map/ppermute | solution.py:33
  25.4 24.6 %collective-permute-start.2 = (bf16[4,6,1,512]{3,2,1,0:T(2,128)(2,1)S(1)}, bf16[4,6,1,512]{3,2,1,0:T(2,128)(2,1)S(1)}, u32[]{:S(2)}, u32[]{:S(2)}) collective-permute-start(bf16[4,6,1,512]{3,2,1,0:T(2,128)(2,1)S(1)} %get-tuple-element.46), channel_id=1, source_target_pairs={{0,1},{1,2},{2,3},{3,4},{4,5},{5,6},{6,7},{7,8},{8,9},{9,10},{10,1... | collective-permute-start | bytes 73736 | tf_op jit(solution)/shard_map/ppermute | solution.py:30
  32.3 17.7 %collective-permute-start.3 = (bf16[4,6,1,512]{3,2,1,0:T(2,128)(2,1)S(1)}, bf16[4,6,1,512]{3,2,1,0:T(2,128)(2,1)S(1)}, u32[]{:S(2)}, u32[]{:S(2)}) collective-permute-start(bf16[4,6,1,512]{3,2,1,0:T(2,128)(2,1)S(1)} %get-tuple-element.47), channel_id=1, source_target_pairs={{1,0},{2,1},{3,2},{4,3},{5,4},{6,5},{7,6},{8,7},{9,8},{10,9},{11,1... | collective-permute-start | bytes 73736 | tf_op jit(solution)/shard_map/ppermute | solution.py:33
  34.8 15.2 %collective-permute-start.6 = (bf16[4,6,1,512]{3,2,1,0:T(2,128)(2,1)S(1)}, bf16[4,6,1,512]{3,2,1,0:T(2,128)(2,1)S(1)}, u32[]{:S(2)}, u32[]{:S(2)}) collective-permute-start(bf16[4,6,1,512]{3,2,1,0:T(2,128)(2,1)S(1)} %get-tuple-element.35), channel_id=1, source_target_pairs={{0,1},{1,2},{2,3},{3,4},{4,5},{5,6},{6,7},{7,8},{8,9},{9,10},{10,1... | collective-permute-start | bytes 73736 | tf_op jit(solution)/shard_map/ppermute | solution.py:30
  39.6 15.4 %collective-permute-start.7 = (bf16[4,6,1,512]{3,2,1,0:T(2,128)(2,1)S(1)}, bf16[4,6,1,512]{3,2,1,0:T(2,128)(2,1)S(1)}, u32[]{:S(2)}, u32[]{:S(2)}) collective-permute-start(bf16[4,6,1,512]{3,2,1,0:T(2,128)(2,1)S(1)} %get-tuple-element.36), channel_id=1, source_target_pairs={{1,0},{2,1},{3,2},{4,3},{5,4},{6,5},{7,6},{8,7},{9,8},{10,9},{11,1... | collective-permute-start | bytes 73736 | tf_op jit(solution)/shard_map/ppermute | solution.py:33
  50.0 7.7 %copy-start.5 = (bf16[4,4,90,512]{3,1,2,0:T(4,128)(2,1)S(1)}, bf16[4,4,90,512]{3,1,2,0:T(4,128)(2,1)}, u32[]{:S(2)}) copy-start(bf16[4,4,90,512]{3,1,2,0:T(4,128)(2,1)} %param.6) | copy-start | bytes 4423684
  76.0 284.4 %all-gather.3.cloned.1.call-start = ((), (), s32[]{:S(2)}) async-start(), calls=%async_computation.4 | async-start | bytes 5308416 | tf_op jit(solution)/shard_map/all_gather | solution.py:138
  300.0 121.2 %all-gather.5.cloned.1.call-start = ((), (), s32[]{:S(2)}) async-start(), calls=%async_computation.6 | async-start | bytes 5308416 | tf_op jit(solution)/shard_map/all_gather | solution.py:161
  331.9 4.2 copy-start.2
  337.4 5.1 %copy-start.1 = (bf16[4,4,90,512]{3,2,1,0:T(8,128)(2,1)S(1)}, bf16[4,4,90,512]{3,2,1,0:T(8,128)(2,1)}, u32[]{:S(2)}) copy-start(bf16[4,4,90,512]{3,2,1,0:T(8,128)(2,1)} %get-tuple-element.40) | copy-start | bytes 4423684
  343.8 5.1 %copy-start = (bf16[4,4,90,512]{3,2,1,0:T(8,128)(2,1)S(1)}, bf16[4,4,90,512]{3,2,1,0:T(8,128)(2,1)}, u32[]{:S(2)}) copy-start(bf16[4,4,90,512]{3,2,1,0:T(8,128)(2,1)} %get-tuple-element.37) | copy-start | bytes 4423684
  350.2 12.4 %copy-start.13 = (bf16[1440,512]{1,0:T(8,128)(2,1)S(1)}, bf16[1440,512]{1,0:T(8,128)(2,1)}, u32[]{:S(2)}) copy-start(bf16[1440,512]{1,0:T(8,128)(2,1)} %reshape.77) | copy-start | bytes 4423684
  360.4 2.5 copy-start.14
  362.9 1.4 copy-start.12
  364.3 1.4 copy-start.11
  365.7 1.4 copy-start.10
  367.0 1.4 copy-start.9
  368.4 1.4 copy-start.8
  (2 other events, 2.7 us)
Sparse Core Ops, SparseCore 0:
  76.1 108.1 reduce-scatter.1
  300.1 60.2 all-gather.2
  362.2 58.9 all-gather.4
where the time goes:
time: 441 us; the launch traced here: 433 us
  waiting for transfers between devices  169 us (38%)
  blocking collectives  130 us (29%)
  local copies, waits for them, and re-layouts  52.8 us (12%)
  starting transfers between devices  30.3 us (7%)
  matrix products  28.2 us (6%)
  between operations  15.2 us (3%)
  other arithmetic  6.7 us (2%)
    reduce_scatter x1, waiting for transfers between devices, per_device(): lax.psum_scatter(term_maker(jnp.int32(0), lax.axis_size(LAT) * (shard_row...  108 us
    all_to_all x2, blocking collectives, sent_to_all(): return lax.all_to_all(copies, axis, split_axis=0, concat_axis=0, tiled=True)  46.8 us
    all_gather x1, waiting for transfers between devices, per_device(): new_weights = lax.all_gather(lon_block, LAT, axis=0, tiled=True)  45 us
    all_to_all x1, blocking collectives, sent_and_summed(): parts = lax.all_to_all(split_up(shard, dim, count), axis, 0, 0, tiled=True)  42.6 us
    psum x5, blocking collectives, by_axis(): return functools.reduce(lax.psum, axes, shard)  41 us
    reshape x9, local copies, waits for them, and re-layouts, pull_product(): windows.append(grad_wide[:, 2 - row_off:2 - row_off + lat_rows, 2 - col_o...  18.3 us
    dot_general x9, matrix products, input_compute(): lax.dot_general(tap_slab, grad_flat, (((0,), (0,)), ((), ())), preferred_...  18.3 us
    ppermute x4, starting transfers between devices, padded(): lax.ppermute(lax.slice_in_dim(block, 0, width, axis=dim), axis, backward)  16.4 us
  transfers between devices with their start and end apart: 11, of which 5 were waited for; matrix products, arithmetic and copies ran while one was open for 11% of the time, Pallas kernels for 0%

commit v1 on v0

--- a/solution.py
+++ b/solution.py
@@ -158,7 +158,10 @@
     )
     new_half = new_master.astype(jnp.bfloat16)
     lon_block = gathered_copies(new_half, LON, 0)
-    new_weights = lax.all_gather(lon_block, LAT, axis=0, tiled=True)
+    size = lax.axis_size(LAT)
+    pieces = jnp.stack([lon_block for _ in range(size)])
+    pieces = lax.all_to_all(pieces, LAT, split_axis=0, concat_axis=0)
+    new_weights = jnp.concatenate(pieces, axis=0)
     return (input_grad, new_weights, new_master, new_one, new_two, grad_scaled)
 
 

time: 441 us -> 458 us (1.039)
  waiting for transfers between devices: 169 us -> 178 us
  starting transfers between devices: 30.3 us -> 35.8 us
    all_to_all x0 -> x1, waiting for transfers between devices: none -> 64.2 us  [per_device(): pieces = lax.all_to_all(pieces, LAT, split_axis=0, concat_axis=0)]
    all_gather x1 -> x0, waiting for transfers between devices: 45 us -> none  [per_device(): new_weights = lax.all_gather(lon_block, LAT, axis=0, tiled=True)]
    all_gather x1, waiting for transfers between devices: 10.2 us -> 0.01 us  [per_device(): lax.all_gather(old_block, LAT, axis=0, tiled=True)]
    all_to_all x0 -> x1, local copies, waits for them, and re-layouts: none -> 5.1 us  [per_device(): pieces = lax.all_to_all(pieces, LAT, split_axis=0, concat_axis=0)]
    all_to_all x0 -> x1, starting transfers between devices: none -> 4.79 us  [per_device(): pieces = lax.all_to_all(pieces, LAT, split_axis=0, concat_axis=0)]
    unnamed x40 -> x39, local copies, waits for them, and re-layouts: 15.4 us -> 11 us
  transfers between devices with their start and end apart: 11 -> 11, of which waited for: 5 -> 4; matrix products, arithmetic and copies ran while one was open for 11% -> 9% of each run, Pallas kernels for 0% -> 0%
where the time goes in v1:
time: 458 us; the launch traced here: 450 us
  waiting for transfers between devices  178 us (39%)
  blocking collectives  130 us (28%)
  local copies, waits for them, and re-layouts  55.4 us (12%)
  starting transfers between devices  35.8 us (8%)
  matrix products  28.2 us (6%)
  between operations  15.5 us (3%)
  other arithmetic  6.7 us (1%)
    reduce_scatter x1, waiting for transfers between devices, per_device(): lax.psum_scatter(term_maker(jnp.int32(0), lax.axis_size(LAT) * (shard_row...  108 us
    all_to_all x1, waiting for transfers between devices, per_device(): pieces = lax.all_to_all(pieces, LAT, split_axis=0, concat_axis=0)  64.2 us
    all_to_all x2, blocking collectives, sent_to_all(): return lax.all_to_all(copies, axis, split_axis=0, concat_axis=0, tiled=True)  46.9 us
    all_to_all x1, blocking collectives, sent_and_summed(): parts = lax.all_to_all(split_up(shard, dim, count), axis, 0, 0, tiled=True)  42.6 us
    psum x5, blocking collectives, by_axis(): return functools.reduce(lax.psum, axes, shard)  41 us
    dot_general x9, matrix products, input_compute(): lax.dot_general(tap_slab, grad_flat, (((0,), (0,)), ((), ())), preferred_...  18.3 us
    reshape x9, local copies, waits for them, and re-layouts, pull_product(): windows.append(grad_wide[:, 2 - row_off:2 - row_off + lat_rows, 2 - col_o...  18.2 us
    ppermute x4, starting transfers between devices, padded(): lax.ppermute(lax.slice_in_dim(block, 0, width, axis=dim), axis, backward)  17.1 us
  transfers between devices with their start and end apart: 11, of which 4 were waited for; matrix products, arithmetic and copies ran while one was open for 9% of the time, Pallas kernels for 0%

profile of v1, /device:TPU:1, one launch (start us, length us, event | category | flops | bytes accessed | tf_op | source)
XLA Modules:
  0.0 450.4 jit_solution(6670414009180385931)
XLA Ops:
  7.2 3.2 fusion.90
  18.4 3.6 collective-permute-start.5
  25.4 6.9 %collective-permute-start.2 = (bf16[4,6,1,512]{3,2,1,0:T(2,128)(2,1)S(1)}, bf16[4,6,1,512]{3,2,1,0:T(2,128)(2,1)S(1)}, u32[]{:S(2)}, u32[]{:S(2)}) collective-permute-start(bf16[4,6,1,512]{3,2,1,0:T(2,128)(2,1)S(1)} %get-tuple-element.46), channel_id=1, source_target_pairs={{0,1},{1,2},{2,3},{3,4},{4,5},{5,6},{6,7},{7,8},{8,9},{9,10},{10,1... | collective-permute-start | bytes 73736 | tf_op jit(solution)/shard_map/ppermute | solution.py:30
  34.8 4.8 %collective-permute-start.6 = (bf16[4,6,1,512]{3,2,1,0:T(2,128)(2,1)S(1)}, bf16[4,6,1,512]{3,2,1,0:T(2,128)(2,1)S(1)}, u32[]{:S(2)}, u32[]{:S(2)}) collective-permute-start(bf16[4,6,1,512]{3,2,1,0:T(2,128)(2,1)S(1)} %get-tuple-element.35), channel_id=1, source_target_pairs={{0,1},{1,2},{2,3},{3,4},{4,5},{5,6},{6,7},{7,8},{8,9},{9,10},{10,1... | collective-permute-start | bytes 73736 | tf_op jit(solution)/shard_map/ppermute | solution.py:30
  39.6 11.1 %collective-permute-start.7 = (bf16[4,6,1,512]{3,2,1,0:T(2,128)(2,1)S(1)}, bf16[4,6,1,512]{3,2,1,0:T(2,128)(2,1)S(1)}, u32[]{:S(2)}, u32[]{:S(2)}) collective-permute-start(bf16[4,6,1,512]{3,2,1,0:T(2,128)(2,1)S(1)} %get-tuple-element.36), channel_id=1, source_target_pairs={{1,0},{2,1},{3,2},{4,3},{5,4},{6,5},{7,6},{8,7},{9,8},{10,9},{11,1... | collective-permute-start | bytes 73736 | tf_op jit(solution)/shard_map/ppermute | solution.py:33
  50.8 4.9 %collective-permute-done.7 = bf16[4,6,1,512]{3,2,1,0:T(2,128)(2,1)S(1)} collective-permute-done((bf16[4,6,1,512]{3,2,1,0:T(2,128)(2,1)S(1)}, bf16[4,6,1,512]{3,2,1,0:T(2,128)(2,1)S(1)}, u32[]{:S(2)}, u32[]{:S(2)}) %collective-permute-start.7) | collective-permute-done | bytes 24608 | tf_op jit(solution)/shard_map/ppermute | solution.py:33
  55.8 2.7 maximum_select_fusion.1
  76.8 108.3 %reduce-scatter.2.cloned.1.call-done = f32[64,9,512]{2,0,1:T(8,128)} async-done(((f32[512,9,512]{2,0,1:T(8,128)}), f32[64,9,512]{2,0,1:T(8,128)}) %reduce-scatter.2.cloned.1.call-update) | async-done | bytes 1179664 | tf_op jit(solution)/shard_map/reduce_scatter | solution.py:141
  187.5 42.6 %all_to_all.20 = f32[32,2,9,512]{3,1,2,0:T(2,128)S(1)} all-to-all(f32[32,2,9,512]{3,1,2,0:T(2,128)S(1)} %copy.78), channel_id=1, replica_groups=mesh['lat_0'=2,'lat_1'=4,'lon_0'=8,'lon_1'=2,'lon_2'=2] {'lon_0','lon_1'..., dimensions={0} | all-to-all | bytes 2359296 | tf_op jit(solution)/shard_map/all_to_all | solution.py:61
  232.5 4.4 psum.35
  236.9 6.8 %psum.36 = f32[]{:T(128)} all-reduce(f32[]{:T(128)} %psum.35), channel_id=1, replica_groups=mesh['lat_0'=2,'lat_1'=4,'lon_0'=8,'lon_1'=2,'lon_2'=2] {'lat_1'}, use_global_device_ids=true, to_apply=%region_4.5 | all-reduce | flops 1 | bytes 8 | tf_op jit(solution)/shard_map/psum | solution.py:66
  243.7 12.3 %psum.37 = f32[]{:T(128)} all-reduce(f32[]{:T(128)} %psum.36), channel_id=1, replica_groups=mesh['lat_0'=2,'lat_1'=4,'lon_0'=8,'lon_1'=2,'lon_2'=2] {'lon_0'}, use_global_device_ids=true, to_apply=%region_5.6 | all-reduce | flops 1 | bytes 8 | tf_op jit(solution)/shard_map/psum | solution.py:66
  256.0 5.9 %psum.38 = f32[]{:T(128)} all-reduce(f32[]{:T(128)} %psum.37), channel_id=1, replica_groups=mesh['lat_0'=2,'lat_1'=4,'lon_0'=8,'lon_1'=2,'lon_2'=2] {'lon_1'}, use_global_device_ids=true, to_apply=%region_6.7 | all-reduce | flops 1 | bytes 8 | tf_op jit(solution)/shard_map/psum | solution.py:66
  261.9 11.5 %psum.39 = f32[]{:T(128)} all-reduce(f32[]{:T(128)} %psum.38), channel_id=1, replica_groups=mesh['lat_0'=2,'lat_1'=4,'lon_0'=8,'lon_1'=2,'lon_2'=2] {'lon_2'}, use_global_device_ids=true, to_apply=%region_7.8 | all-reduce | flops 1 | bytes 8 | tf_op jit(solution)/shard_map/psum | solution.py:66
  276.1 23.0 %all_to_all.21 = bf16[32,2,9,512]{3,1,2,0:T(2,128)(2,1)S(1)} all-to-all(bf16[32,2,9,512]{3,1,2,0:T(2,128)(2,1)S(1)} %broadcast_in_dim.24), channel_id=1, replica_groups=mesh['lat_0'=2,'lat_1'=4,'lon_0'=8,'lon_1'=2,'lon_2'=2] {'lon_0','lon_1'..., dimensions={0} | all-to-all | bytes 1179648 | tf_op jit(solution)/shard_map/all_to_all | solution.py:40
  301.0 23.9 %all_to_all.22 = bf16[32,2,9,512]{3,1,2,0:T(2,128)(2,1)S(1)} all-to-all(bf16[32,2,9,512]{3,1,2,0:T(2,128)(2,1)S(1)} %broadcast_in_dim.25), channel_id=1, replica_groups=mesh['lat_0'=2,'lat_1'=4,'lon_0'=8,'lon_1'=2,'lon_2'=2] {'lon_0','lon_1'..., dimensions={0} | all-to-all | bytes 1179648 | tf_op jit(solution)/shard_map/all_to_all | solution.py:40
  325.6 2.8 stack.43
  328.3 4.8 %all-to-all-start.3 = ((bf16[8,64,9,512]{3,1,2,0:T(8,128)(2,1)}), bf16[8,64,9,512]{3,1,2,0:T(8,128)(2,1)}, u32[]{:S(2)}, u32[]{:S(2)}) async-start(bf16[8,64,9,512]{3,1,2,0:T(8,128)(2,1)} %stack.43), calls=%async_computation.4 | async-start | bytes 9437184 | tf_op jit(solution)/shard_map/all_to_all | solution.py:163
  333.1 6.3 %fusion.87 = (bf16[4,4,90,512]{3,2,1,0:T(8,128)(2,1)}, bf16[4,4,90,512]{3,2,1,0:T(8,128)(2,1)}, bf16[4,4,90,512]{3,2,1,0:T(8,128)(2,1)}, bf16[4,4,90,512]{3,2,1,...) fusion(bf16[4,6,92,512]{3,2,1,0:T(8,128)(2,1)S(1)} %get-tuple-e, ...), kind=kLoop, calls=%fused_computation.81 | loop fusion | bytes 26542080 | tf_op jit(solution)/shard_map/slice | solution.py:86
  344.9 2.6 reshape.81
  347.5 2.5 reshape.82
  351.3 2.6 reshape.84
  357.6 64.2 %all-to-all-done.3 = bf16[8,64,9,512]{3,1,2,0:T(8,128)(2,1)} async-done(((bf16[8,64,9,512]{3,1,2,0:T(8,128)(2,1)}), bf16[8,64,9,512]{3,1,2,0:T(8,128)(2,1)}, u32[]{:S(2)}, u32[]{:S(2)}) %all-to-all-start.3) | async-done | bytes 4718624 | tf_op jit(solution)/shard_map/all_to_all | solution.py:163
  421.8 5.1 %copy.80 = bf16[8,64,9,512]{3,1,0,2:T(8,128)(2,1)} copy(bf16[8,64,9,512]{3,1,2,0:T(8,128)(2,1)} %all-to-all-done.3) | data formatting | bytes 9437184 | tf_op jit(solution)/shard_map/all_to_all | solution.py:163
  (97 shorter events, 68.1 us)
Async XLA Ops:
  7.2 9.4 %copy-start.3 = (bf16[4,4,90,512]{3,1,2,0:T(4,128)(2,1)S(1)}, bf16[4,4,90,512]{3,1,2,0:T(4,128)(2,1)}, u32[]{:S(2)}) copy-start(bf16[4,4,90,512]{3,1,2,0:T(4,128)(2,1)} %param.5) | copy-start | bytes 4423684
  7.2 177.9 %reduce-scatter.2.cloned.1.call-start = ((), (), s32[]{:S(2)}) async-start(), calls=%async_computation.6 | async-start | bytes 10616832 | tf_op jit(solution)/shard_map/reduce_scatter | solution.py:141
  11.2 11.7 %collective-permute-start = (bf16[4,1,90,512]{3,2,1,0:T(8,128)(2,1)}, bf16[4,1,90,512]{3,2,1,0:T(8,128)(2,1)}, u32[]{:S(2)}, u32[]{:S(2)}) collective-permute-start(bf16[4,1,90,512]{3,2,1,0:T(8,128)(2,1)} %copy.111), channel_id=1, source_target_pairs={{0,32},{32,64},{64,96},{96,128},{128,160},{160,192},{192,224},{224... | collective-permute-start | bytes 1105928 | tf_op jit(solution)/shard_map/ppermute | solution.py:30
  14.2 9.8 %copy-start.4 = (bf16[4,4,90,512]{3,1,2,0:T(4,128)(2,1)S(1)}, bf16[4,4,90,512]{3,1,2,0:T(4,128)(2,1)}, u32[]{:S(2)}) copy-start(bf16[4,4,90,512]{3,1,2,0:T(4,128)(2,1)} %param.6) | copy-start | bytes 4423684
  14.2 10.1 %collective-permute-start.1 = (bf16[4,1,90,512]{3,2,1,0:T(8,128)(2,1)}, bf16[4,1,90,512]{3,2,1,0:T(8,128)(2,1)}, u32[]{:S(2)}, u32[]{:S(2)}) collective-permute-start(bf16[4,1,90,512]{3,2,1,0:T(8,128)(2,1)} %copy.112), channel_id=1, source_target_pairs={{32,0},{64,32},{96,64},{128,96},{160,128},{192,160},{224,192},{0,2... | collective-permute-start | bytes 1105928 | tf_op jit(solution)/shard_map/ppermute | solution.py:33
  18.4 14.0 %collective-permute-start.4 = (bf16[4,1,90,512]{3,2,1,0:T(8,128)(2,1)}, bf16[4,1,90,512]{3,2,1,0:T(8,128)(2,1)}, u32[]{:S(2)}, u32[]{:S(2)}) collective-permute-start(bf16[4,1,90,512]{3,2,1,0:T(8,128)(2,1)} %copy.113), channel_id=1, source_target_pairs={{0,32},{32,64},{64,96},{96,128},{128,160},{160,192},{192,224},{224... | collective-permute-start | bytes 1105928 | tf_op jit(solution)/shard_map/ppermute | solution.py:30
  18.4 15.3 %collective-permute-start.5 = (bf16[4,1,90,512]{3,2,1,0:T(8,128)(2,1)S(1)}, bf16[4,1,90,512]{3,2,1,0:T(8,128)(2,1)}, u32[]{:S(2)}, u32[]{:S(2)}) collective-permute-start(bf16[4,1,90,512]{3,2,1,0:T(8,128)(2,1)S(1)} %copy.114), channel_id=1, source_target_pairs={{32,0},{64,32},{96,64},{128,96},{160,128},{192,160},{224,192},{0,2... | collective-permute-start | bytes 1105928 | tf_op jit(solution)/shard_map/ppermute | solution.py:33
  25.4 25.3 %collective-permute-start.2 = (bf16[4,6,1,512]{3,2,1,0:T(2,128)(2,1)S(1)}, bf16[4,6,1,512]{3,2,1,0:T(2,128)(2,1)S(1)}, u32[]{:S(2)}, u32[]{:S(2)}) collective-permute-start(bf16[4,6,1,512]{3,2,1,0:T(2,128)(2,1)S(1)} %get-tuple-element.46), channel_id=1, source_target_pairs={{0,1},{1,2},{2,3},{3,4},{4,5},{5,6},{6,7},{7,8},{8,9},{9,10},{10,1... | collective-permute-start | bytes 73736 | tf_op jit(solution)/shard_map/ppermute | solution.py:30
  32.3 18.4 %collective-permute-start.3 = (bf16[4,6,1,512]{3,2,1,0:T(2,128)(2,1)S(1)}, bf16[4,6,1,512]{3,2,1,0:T(2,128)(2,1)S(1)}, u32[]{:S(2)}, u32[]{:S(2)}) collective-permute-start(bf16[4,6,1,512]{3,2,1,0:T(2,128)(2,1)S(1)} %get-tuple-element.47), channel_id=1, source_target_pairs={{1,0},{2,1},{3,2},{4,3},{5,4},{6,5},{7,6},{8,7},{9,8},{10,9},{11,1... | collective-permute-start | bytes 73736 | tf_op jit(solution)/shard_map/ppermute | solution.py:33
  34.8 16.0 %collective-permute-start.6 = (bf16[4,6,1,512]{3,2,1,0:T(2,128)(2,1)S(1)}, bf16[4,6,1,512]{3,2,1,0:T(2,128)(2,1)S(1)}, u32[]{:S(2)}, u32[]{:S(2)}) collective-permute-start(bf16[4,6,1,512]{3,2,1,0:T(2,128)(2,1)S(1)} %get-tuple-element.35), channel_id=1, source_target_pairs={{0,1},{1,2},{2,3},{3,4},{4,5},{5,6},{6,7},{7,8},{8,9},{9,10},{10,1... | collective-permute-start | bytes 73736 | tf_op jit(solution)/shard_map/ppermute | solution.py:30
  39.6 16.1 %collective-permute-start.7 = (bf16[4,6,1,512]{3,2,1,0:T(2,128)(2,1)S(1)}, bf16[4,6,1,512]{3,2,1,0:T(2,128)(2,1)S(1)}, u32[]{:S(2)}, u32[]{:S(2)}) collective-permute-start(bf16[4,6,1,512]{3,2,1,0:T(2,128)(2,1)S(1)} %get-tuple-element.36), channel_id=1, source_target_pairs={{1,0},{2,1},{3,2},{4,3},{5,4},{6,5},{7,6},{8,7},{9,8},{10,9},{11,1... | collective-permute-start | bytes 73736 | tf_op jit(solution)/shard_map/ppermute | solution.py:33
  50.8 7.7 %copy-start.5 = (bf16[4,4,90,512]{3,1,2,0:T(4,128)(2,1)S(1)}, bf16[4,4,90,512]{3,1,2,0:T(4,128)(2,1)}, u32[]{:S(2)}) copy-start(bf16[4,4,90,512]{3,1,2,0:T(4,128)(2,1)} %param.6) | copy-start | bytes 4423684
  76.7 350.2 %all-gather.2.cloned.1.call-start = ((), (), s32[]{:S(2)}) async-start(), calls=%async_computation.5 | async-start | bytes 5308416 | tf_op jit(solution)/shard_map/all_gather | solution.py:138
  328.3 93.5 %all-to-all-start.3 = ((bf16[8,64,9,512]{3,1,2,0:T(8,128)(2,1)}), bf16[8,64,9,512]{3,1,2,0:T(8,128)(2,1)}, u32[]{:S(2)}, u32[]{:S(2)}) async-start(bf16[8,64,9,512]{3,1,2,0:T(8,128)(2,1)} %stack.43), calls=%async_computation.4 | async-start | bytes 9437184 | tf_op jit(solution)/shard_map/all_to_all | solution.py:163
  339.4 4.2 copy-start.2
  344.9 5.1 %copy-start.1 = (bf16[4,4,90,512]{3,2,1,0:T(8,128)(2,1)S(1)}, bf16[4,4,90,512]{3,2,1,0:T(8,128)(2,1)}, u32[]{:S(2)}) copy-start(bf16[4,4,90,512]{3,2,1,0:T(8,128)(2,1)} %get-tuple-element.40) | copy-start | bytes 4423684
  351.3 5.0 %copy-start = (bf16[4,4,90,512]{3,2,1,0:T(8,128)(2,1)S(1)}, bf16[4,4,90,512]{3,2,1,0:T(8,128)(2,1)}, u32[]{:S(2)}) copy-start(bf16[4,4,90,512]{3,2,1,0:T(8,128)(2,1)} %get-tuple-element.37) | copy-start | bytes 4423684
  427.0 2.2 copy-start.13
  427.0 2.9 copy-start.14
  429.9 1.4 copy-start.12
  431.3 1.4 copy-start.11
  432.6 1.4 copy-start.10
  434.0 1.4 copy-start.9
  435.4 1.4 copy-start.8
  (2 other events, 2.7 us)
Sparse Core Ops, SparseCore 0:
  76.9 108.1 reduce-scatter.1
  300.8 102.7 all-gather.1
